TPU v7x, 32 devices: a whole 2x2x4 slice. The times are simulated.
32 devices in a mesh: patch: 16 (over z, y, x), width: 2 (over core).
Axes of the slice: x: 2, y: 2, z: 4, core: 2. Of those that a mesh axis runs over, the one named last changes fastest.
Arguments:
- node_latents: bfloat16 [512, 2048], P('width', 'patch'), may hold values from -6 to 6
- edge_latents: bfloat16 [512, 16384], P('width', 'patch'), may hold values from -6 to 6
- senders: int32 [16384], P('patch'), may hold values from 0 to 2047, as said below
- receivers: int32 [16384], P('patch'), may hold values from 0 to 2047, as said below
- edge_count: int32 [16], P('patch'), may hold values from 512 to 1024, as said below
- edge_in_weight: bfloat16 [2, 512, 1536], P(None, 'width'), may hold values from -0.15625 to 0.15625
- edge_in_bias: float32 [2, 512], P(None, 'width'), may hold values from -3 to 3
- edge_out_weight: bfloat16 [2, 512, 512], P(None, 'width'), may hold values from -0.25 to 0.25
- edge_out_bias: float32 [2, 512], P(None, 'width'), may hold values from -3 to 3
- edge_gain: float32 [2, 512], P(None, 'width'), may hold values from 0.1 to 1.9
- edge_shift: float32 [2, 512], P(None, 'width'), may hold values from -3 to 3
- node_in_weight: bfloat16 [2, 512, 1024], P(None, 'width'), may hold values from -0.1875 to 0.1875
- node_in_bias: float32 [2, 512], P(None, 'width'), may hold values from -3 to 3
- node_out_weight: bfloat16 [2, 512, 512], P(None, 'width'), may hold values from -0.25 to 0.25
- node_out_bias: float32 [2, 512], P(None, 'width'), may hold values from -3 to 3
- node_gain: float32 [2, 512], P(None, 'width'), may hold values from 0.1 to 1.9
- node_shift: float32 [2, 512], P(None, 'width'), may hold values from -3 to 3
Outputs:
- nodes_out: bfloat16 [512, 2048], P('width', 'patch')
- edges_out: bfloat16 [512, 16384], P('width', 'patch')
Inputs may be any that keep to these rules, and one draw needn't show every extreme that they name: `senders`: the sender of a slot of patch p is a node of patch p, of patch p - 1 or p + 1 (counted around, modulo the number of patches), or one of the first 16 nodes of some patch. `receivers`: row r names a node of patch r // 1024, from (r // 1024) * 128 to that plus 128 - 1. Slots p * 1024 to p * 1024 + edge_count[p] - 1 of patch p are live, the rest are padding; some patch has all 1024 slots live.
All inputs are finite; a program needn't handle non-finite values.
Results may differ from a plain program's by a relative error of at most 0.014.
Values may be sent and summed in bfloat16 or wider, within the bound.
A program may use at most 64 MiB of HBM per device.

v0:
```python
import functools

import jax
import jax.numpy as jnp
from jax import lax
from jax.experimental import pallas as pl
from jax.experimental.pallas import tpu as pltpu
from jax.sharding import PartitionSpec as P

MESH = pl.DeviceIdType.MESH
epsilon = 1e-05
bf16 = jnp.bfloat16
f32 = jnp.float32


def dot(left, right, dims=((1,), (0,))):
    return lax.dot_general(left, right, (dims, ((), ())), preferred_element_type=f32)


def silu(v):
    h = 0.5 * v
    return h + h * jnp.tanh(h)


def layer_norm(values, gain, shift):
    width = values.shape[0]
    mean = jnp.sum(values, axis=0, keepdims=True) / width
    square = jnp.sum(values * values, axis=0, keepdims=True) / width
    return (values - mean) * lax.rsqrt(square - mean * mean + epsilon) * gain + shift


def kernel(
    patches,
    nodes_in,
    edges_in,
    senders_in,
    receivers_in,
    count_in,
    wi_in,
    wo_in,
    vi_in,
    vo_in,
    *rest,
):
    vector_in = rest[:8]
    nodes_out, edges_out = rest[8:10]
    (
        nodes,
        edges,
        wi,
        wo,
        vi,
        vo,
        vectors,
        columns,
        halo,
        coarse,
        part_send,
        coarse_send,
        agg_send,
        agg_recv,
        own,
        table,
        hot_own,
        hot_far,
        incidence,
        before,
        senders_ref,
        receivers_ref,
        count_ref,
        wo_turned,
        vo_turned,
        graph_sem,
        local_sem,
        w_send,
        w_recv,
        halo_send,
        halo_recv,
        coarse_send_sem,
        coarse_recv_sem,
        relay_send,
        relay_recv,
        agg_sems,
        out_sems,
    ) = rest[10:]
    layers = wi.shape[0]
    half = nodes_in.shape[0]
    width = 2 * half
    rows = nodes_in.shape[1]
    slots = edges_in.shape[1]
    mine = slots // 2
    top = coarse_send.shape[1]
    far = patches - 3

    me = lax.axis_index("patch")
    core = lax.axis_index("width")
    other = 1 - core
    here = pl.ds(pl.multiple_of(core * half, half), half)
    there = pl.ds(pl.multiple_of(other * half, half), half)
    my_slots = pl.ds(pl.multiple_of(core * mine, mine), mine)
    other_slots = pl.ds(pl.multiple_of(other * mine, mine), mine)

    def local(src, dst, index):
        return pltpu.make_async_copy(src, dst, local_sem.at[index])

    def remote(src, dst, send, recv, patch, width_index):
        return pltpu.make_async_remote_copy(
            src_ref=src,
            dst_ref=dst,
            send_sem=send,
            recv_sem=recv,
            device_id={"patch": patch, "width": width_index},
            device_id_type=MESH,
        )

    blocks = [
        (nodes_in, nodes.at[here], nodes_in, nodes.at[there]),
        (edges_in.at[:, my_slots], edges.at[here], edges_in.at[:, other_slots], edges.at[there]),
    ]
    place = {"nodes": 0, "edges": 1}
    for layer in range(layers):
        for name, source, target in (("wi", wi_in, wi), ("wo", wo_in, wo), ("vi", vi_in, vi), ("vo", vo_in, vo)):
            place[name, layer] = len(blocks)
            blocks.append(
                (source.at[layer], target.at[layer, here], source.at[layer], target.at[layer, there])
            )
        if layer == 0:
            place["vectors"] = len(blocks)
            for index, source in enumerate(vector_in):
                blocks.append(
                    (source, vectors.at[index, :, here], source, vectors.at[index, :, there])
                )

    def greet(step, carry):
        target = lax.rem(me + step, patches)
        pl.semaphore_signal(
            pltpu.get_barrier_semaphore(), inc=1, device_id={"patch": target, "width": core}, device_id_type=MESH
        )
        return carry

    barrier = pltpu.get_barrier_semaphore()
    pl.semaphore_signal(barrier, inc=1, device_id={"patch": me, "width": other}, device_id_type=MESH)
    lax.fori_loop(1, patches, greet, 0)

    graph = [
        pltpu.make_async_copy(source, target, graph_sem.at[i])
        for i, (source, target) in enumerate(
            ((senders_in, senders_ref), (receivers_in, receivers_ref), (count_in, count_ref))
        )
    ]
    locals_ = [local(b[0], b[1], i) for i, b in enumerate(blocks)]
    locals_[0].start()
    for copy in graph + locals_[1:]:
        copy.start()
    locals_[0].wait()
    coarse_send[0] = nodes[here, :].astype(f32).T[:top].astype(bf16)
    for copy in graph:
        copy.wait()

    sender = senders_ref[:, my_slots]
    receiver = receivers_ref[:, my_slots] - me * rows
    slot = lax.broadcasted_iota(jnp.int32, (1, mine), 1) + core * mine
    live = slot < count_ref[0]
    owner = sender // rows
    within = sender - owner * rows
    distance = lax.rem(me - owner + patches, patches)
    node_iota = lax.broadcasted_iota(jnp.int32, (rows, mine), 0)

    def hot(index, iota):
        return jnp.where(iota == index, 1.0, 0.0).astype(bf16)

    hot_own[:rows] = hot(jnp.where(distance == 0, within, -1), node_iota)
    hot_own[rows:] = hot(receiver, node_iota)
    hot_far[:rows] = hot(jnp.where(distance == 1, within, -1), node_iota)
    hot_far[rows : 2 * rows] = hot(jnp.where(distance == patches - 1, within, -1), node_iota)
    far_index = jnp.where((distance >= 2) & (distance <= patches - 2), (distance - 2) * top + within, -1)
    hot_far[2 * rows :] = hot(far_index, lax.broadcasted_iota(jnp.int32, (coarse.shape[2], mine), 0))
    incidence[...] = hot(jnp.where(live, receiver, -1), node_iota)
    pad = coarse.shape[2] - far * top
    if pad:
        for layer in range(layers):
            for part in range(2):
                coarse[layer, part, far * top :, :] = jnp.zeros((pad, half), bf16)

    pl.semaphore_wait(barrier, patches)

    def send_far(layer, source):
        copies = [
            remote(
                source,
                halo.at[layer, here, pl.ds(side * rows, rows)],
                halo_send.at[layer, side],
                halo_recv.at[layer, side],
                lax.rem(me + step, patches),
                core,
            )
            for side, step in enumerate((1, patches - 1))
        ]
        for copy in copies:
            copy.start()
        return copies

    def spread_coarse(layer):
        def spread(step, carry):
            remote(
                coarse_send.at[layer],
                coarse.at[layer, core, pl.ds(pl.multiple_of((step - 2) * top, top), top)],
                coarse_send_sem.at[layer],
                coarse_recv_sem.at[layer],
                lax.rem(me + step, patches),
                core,
            ).start()
            return carry

        lax.fori_loop(2, patches - 1, spread, 0)

    sent_far = send_far(0, nodes.at[here])
    spread_coarse(0)
    remotes = [
        remote(b[2], b[1], w_send.at[i], w_recv.at[i], me, other) for i, b in enumerate(blocks)
    ]
    for copy in remotes:
        copy.start()

    def arrive(index):
        if index:
            locals_[index].wait()
        b = blocks[index]
        remote(b[3], b[3], w_send.at[index], w_recv.at[index], me, other).wait_recv()

    def column(index, layer):
        position = index * layers + layer
        return columns[:, position : position + 1]

    waited_out = []
    sender_columns = slice(width, 2 * width)
    wide = [(k * mine // 2, (k + 1) * mine // 2) for k in range(2)]
    for layer in range(layers):
        if layer:
            arrive(place["wi", layer])
            part = dot(wi[layer, here, sender_columns], nodes[...])
            part_send[layer] = part.astype(bf16)
            sent_far = send_far(layer, part_send.at[layer])
            coarse_send[layer] = part.T[:top].astype(bf16)
            spread_coarse(layer)
        else:
            arrive(place["nodes"])
            arrive(place["wi", layer])

        own[:, :rows] = dot(wi[layer, :, sender_columns], nodes[...]).astype(bf16)
        own[:, rows:] = dot(wi[layer, :, 2 * width :], nodes[...]).astype(bf16)
        if layer == 0:
            arrive(place["edges"])
            for k in range(8):
                arrive(place["vectors"] + k)
            flat = vectors[...].reshape(8 * layers, width)
            columns[...] = flat.T
        before[...] = (
            dot(wi[layer, :, :width], edges[...]) + dot(own[...], hot_own[...]) + column(0, layer)
        )
        arrive(place["vi", layer])
        node_first = dot(vi[layer, :, :width], nodes[...]) + column(4, layer)
        arrive(place["wo", layer])
        wo_turned[...] = wo[layer].T
        arrive(place["vo", layer])
        vo_turned[...] = vo[layer].T

        relays = []

        def passed(index, ref):
            return remote(ref, ref, relay_send.at[layer, index], relay_recv.at[layer, index], me, other)

        for side in range(2):
            sent_far[side].wait_recv()
            relays.append(passed(side, halo.at[layer, here, pl.ds(side * rows, rows)]))
            relays[-1].start()
        every = coarse.at[layer, core, pl.ds(0, far * top)]
        all_coarse = remote(every, every, coarse_send_sem.at[layer], coarse_recv_sem.at[layer], me, other)
        all_coarse.wait_recv()
        relays.append(passed(2, every))
        relays[-1].start()

        if layer == 0:
            senders_here = wi[layer, :, pl.ds(pl.multiple_of(width + core * half, half), half)]
            senders_there = wi[layer, :, pl.ds(pl.multiple_of(width + other * half, half), half)]
            table[:, : 2 * rows] = dot(senders_here, halo[layer, here, :])
            table[:, 2 * rows :] = dot(senders_here, coarse[layer, core], ((1,), (1,)))
        else:
            before[here, :] = (
                before[here, :]
                + dot(halo[layer, here, :], hot_far[: 2 * rows])
                + dot(coarse[layer, core], hot_far[2 * rows :], ((0,), (0,)))
            )
        for side in range(2):
            passed(side, halo.at[layer, there, pl.ds(side * rows, rows)]).wait_recv()
        passed(2, coarse.at[layer, other, pl.ds(0, far * top)]).wait_recv()
        if layer == 0:
            near = (table[:, : 2 * rows] + dot(senders_there, halo[layer, there, :])).astype(bf16)
            away = (
                table[:, 2 * rows :] + dot(senders_there, coarse[layer, other], ((1,), (1,)))
            ).astype(bf16)
        else:
            before[there, :] = (
                before[there, :]
                + dot(halo[layer, there, :], hot_far[: 2 * rows])
                + dot(coarse[layer, other], hot_far[2 * rows :], ((0,), (0,)))
            )

        partial = None
        for low, high in wide:
            value = before[:, low:high]
            if layer == 0:
                value = (
                    value
                    + dot(near, hot_far[: 2 * rows, low:high])
                    + dot(away, hot_far[2 * rows :, low:high])
                )
            hidden = silu(value).astype(bf16)
            mlp = dot(wo_turned[...], hidden) + column(1, layer)
            updated = edges[:, low:high].astype(f32) + layer_norm(mlp, column(2, layer), column(3, layer))
            fresh = jnp.where(live[:, low:high], updated, 0.0).astype(bf16)
            edges[:, low:high] = fresh
            term = dot(fresh, incidence[:, low:high], ((1,), (1,)))
            partial = term if partial is None else partial + term
        agg_send[layer] = partial.astype(bf16)
        swap = remote(
            agg_send.at[layer], agg_recv.at[layer], agg_sems.at[layer, 0], agg_sems.at[layer, 1], me, other
        )
        swap.start()
        if layer == layers - 1:
            keep = pltpu.make_async_copy(edges.at[here], edges_out.at[:, my_slots], out_sems.at[0])
            keep.start()
            give = remote(
                edges.at[there], edges_out.at[:, my_slots], out_sems.at[1], out_sems.at[2], me, other
            )
            give.start()
        swap.wait_recv()
        aggregate = (partial + agg_recv[layer].astype(f32)).astype(bf16)
        node_hidden = silu(node_first + dot(vi[layer, :, width:], aggregate)).astype(bf16)
        node_mlp = dot(vo_turned[...], node_hidden) + column(5, layer)
        for copy in sent_far:
            copy.wait_send()
        nodes[...] = (
            nodes[...].astype(f32) + layer_norm(node_mlp, column(6, layer), column(7, layer))
        ).astype(bf16)
        waited_out += [all_coarse] + relays + [swap]

    nodes_out[...] = nodes[here, :]
    for copy in remotes + waited_out:
        copy.wait_send()
    keep.wait()
    give.wait_send()
    got = edges_out.at[:, other_slots]
    remote(got, got, out_sems.at[1], out_sems.at[2], me, other).wait_recv()


def put(nodes, edges, nodes_out, edges_out, sems):
    copies = [
        pltpu.make_async_copy(edges, edges_out, sems.at[0]),
        pltpu.make_async_copy(nodes, nodes_out, sems.at[1]),
    ]
    for copy in copies:
        copy.start()
    for copy in copies:
        copy.wait()


def on_device(
    patches,
    node_latents,
    edge_latents,
    senders,
    receivers,
    edge_count,
    edge_in_weight,
    edge_in_bias,
    edge_out_weight,
    edge_out_bias,
    edge_gain,
    edge_shift,
    node_in_weight,
    node_in_bias,
    node_out_weight,
    node_out_bias,
    node_gain,
    node_shift,
):
    half, rows = node_latents.shape
    slots = edge_latents.shape[1]
    layers = edge_in_weight.shape[0]
    width = 2 * half
    mine = slots // 2
    top = rows // 8
    far_rows = -(-(patches - 3) * top // 128) * 128
    vmem = pltpu.VMEM
    dma = pltpu.SemaphoreType.DMA
    copies = 2 + 4 * layers + 8
    anywhere = pl.BlockSpec(memory_space=pl.ANY)
    results = pl.pallas_call(
        functools.partial(kernel, patches),
        out_shape=(
            vmem((half, rows), bf16),
            vmem((half, slots), bf16),
        ),
        in_specs=[anywhere] * 17,
        out_specs=(pl.BlockSpec(memory_space=vmem),) * 2,
        scratch_shapes=[
            vmem((width, rows), bf16),
            vmem((width, mine), bf16),
            vmem((layers, width, 3 * width), bf16),
            vmem((layers, width, width), bf16),
            vmem((layers, width, 2 * width), bf16),
            vmem((layers, width, width), bf16),
            vmem((8, layers, width), f32),
            vmem((width, 8 * layers), f32),
            vmem((layers, width, 2 * rows), bf16),
            vmem((layers, 2, far_rows, half), bf16),
            vmem((layers, half, rows), bf16),
            vmem((layers, top, half), bf16),
            vmem((layers, width, rows), bf16),
            vmem((layers, width, rows), bf16),
            vmem((width, 2 * rows), bf16),
            vmem((width, 2 * rows + far_rows), f32),
            vmem((2 * rows, mine), bf16),
            vmem((2 * rows + far_rows, mine), bf16),
            vmem((rows, mine), bf16),
            vmem((width, mine), f32),
            vmem((1, slots), jnp.int32),
            vmem((1, slots), jnp.int32),
            pltpu.SMEM((1,), jnp.int32),
            vmem((width, width), bf16),
            vmem((width, width), bf16),
            dma((3,)),
            dma((copies,)),
            dma((copies,)),
            dma((copies,)),
            dma((layers, 2)),
            dma((layers, 2)),
            dma((layers,)),
            dma((layers,)),
            dma((layers, 3)),
            dma((layers, 3)),
            dma((layers, 2)),
            dma((3,)),
        ],
        compiler_params=pltpu.CompilerParams(collective_id=0, has_side_effects=True, vmem_limit_bytes=56 * 2**20),
    )(
        node_latents,
        edge_latents,
        senders.reshape(1, slots),
        receivers.reshape(1, slots),
        edge_count,
        edge_in_weight,
        edge_out_weight,
        node_in_weight,
        node_out_weight,
        edge_in_bias,
        edge_out_bias,
        edge_gain,
        edge_shift,
        node_in_bias,
        node_out_bias,
        node_gain,
        node_shift,
    )
    return pl.pallas_call(
        put,
        out_shape=(
            jax.ShapeDtypeStruct((half, rows), bf16),
            jax.ShapeDtypeStruct((half, slots), bf16),
        ),
        in_specs=[pl.BlockSpec(memory_space=vmem)] * 2,
        out_specs=(anywhere, anywhere),
        scratch_shapes=[dma((2,))],
        compiler_params=pltpu.CompilerParams(vmem_limit_bytes=4 * 2**20),
    )(*results)


def solution(mesh):
    by_width = P(None, "width")
    return jax.shard_map(
        functools.partial(on_device, mesh.shape["patch"]),
        mesh=mesh,
        in_specs=(
            P("width", "patch"),
            P("width", "patch"),
            P("patch"),
            P("patch"),
            P("patch"),
            P(None, "width", None),
            by_width,
            P(None, "width", None),
            by_width,
            by_width,
            by_width,
            P(None, "width", None),
            by_width,
            P(None, "width", None),
            by_width,
            by_width,
            by_width,
        ),
        out_specs=(P("width", "patch"), P("width", "patch")),
        check_vma=False,
    )
```

profile of v0, /device:TPU:0, one launch (start us, length us, event | category | flops | bytes accessed | tf_op | source)
XLA Modules:
  0.0 31.4 jit_solution(10473374017637092314)
XLA Ops:
  1.3 29.3 %shard_map.176 = (bf16[256,128]{1,0:T(8,128)(2,1)S(1)}, bf16[256,1024]{1,0:T(8,128)(2,1)S(1)}) custom-call(bf16[256,128]{1,0:T(8,128)(2,1)} %nodes_in.1, bf16[256,1024]{1,0:T(8,128)(2,1)} %edges_in.1, s32[1,1024]{1,0:T(1,128)} %bitcast.2, s32[1,1024]{1,0:T(1,128)} %bitcast.3, s32[1]{0:T(128)S(6)} %copy.19.count_in, bf16[2,256,1536]{2,1,0:T(8,128)(2,1)} %wi_in.1, ...), custom_call_target="tpu_custom_call" | custom-call | tf_op jit(solution)/shard_map/pallas_call | solution.py:399
  30.6 0.8 %shard_map.177 = (bf16[256,128]{1,0:T(8,128)(2,1)}, bf16[256,1024]{1,0:T(8,128)(2,1)}) custom-call(bf16[256,128]{1,0:T(8,128)(2,1)S(1)} %get-tuple-element.4.nodes, bf16[256,1024]{1,0:T(8,128)(2,1)S(1)} %get-tuple-element.5.edges), custom_call_target="tpu_custom_call" | custom-call | tf_op jit(solution)/shard_map/pallas_call | solution.py:466
where the time goes:
time: 31.6 us; the launch traced here: 31.4 us
  Pallas kernels  30.2 us (96%)
  between operations  1.29 us (4%)
    pallas_call x1, Pallas kernels, on_device(): pl.pallas_call(functools.partial(kernel, patches), out_shape=(vmem((half,...  29.3 us
    pallas_call x1, Pallas kernels, on_device(): pl.pallas_call(put, out_shape=(jax.ShapeDtypeStruct((half, rows), bf16),...  0.82 us

commit v1 on v0

v1 whole, which is shorter than its diff:
```python
import functools

import jax
import jax.numpy as jnp
from jax import lax
from jax.experimental import pallas as pl
from jax.experimental.pallas import tpu as pltpu
from jax.sharding import PartitionSpec as P

MESH = pl.DeviceIdType.MESH
epsilon = 1e-05
bf16 = jnp.bfloat16
f32 = jnp.float32


def dot(left, right, dims=((1,), (0,))):
    return lax.dot_general(left, right, (dims, ((), ())), preferred_element_type=f32)


def silu(v):
    h = 0.5 * v
    return h + h * jnp.tanh(h)


def layer_norm(values, gain, shift):
    width = values.shape[0]
    mean = jnp.sum(values, axis=0, keepdims=True) / width
    square = jnp.sum(values * values, axis=0, keepdims=True) / width
    return (values - mean) * lax.rsqrt(square - mean * mean + epsilon) * gain + shift


def kernel(
    patches,
    nodes_in,
    edges_in,
    senders_in,
    receivers_in,
    count_in,
    wi_in,
    wo_in,
    vi_in,
    vo_in,
    *rest,
):
    vector_in = rest[:8]
    nodes_out, edges_out = rest[8:10]
    (
        nodes,
        edges,
        weights,
        vectors,
        columns,
        halo,
        coarse,
        part_send,
        coarse_send,
        agg_send,
        agg_recv,
        partial,
        own,
        hot_own,
        hot_far,
        incidence,
        before,
        graph_ref,
        count_ref,
        wo_turned,
        vo_turned,
        graph_sem,
        local_sem,
        w_send,
        w_recv,
        halo_send,
        halo_recv,
        coarse_send_sem,
        coarse_recv_sem,
        relay_send,
        relay_recv,
        agg_sems,
        out_sems,
        mate,
        all_in,
    ) = rest[10:]
    layers = weights.shape[0]
    half = nodes_in.shape[0]
    width = 2 * half
    rows = nodes_in.shape[1]
    slots = edges_in.shape[1]
    mine = slots // 2
    top = coarse_send.shape[1]
    far = patches - 3
    lead = 1

    me = lax.axis_index("patch")
    odd = lax.rem(me, 2)
    core = lax.axis_index("width")
    other = 1 - core
    here = pl.ds(pl.multiple_of(core * half, half), half)
    there = pl.ds(pl.multiple_of(other * half, half), half)
    my_slots = pl.ds(pl.multiple_of(core * mine, mine), mine)
    other_slots = pl.ds(pl.multiple_of(other * mine, mine), mine)

    def remote(src, dst, send, recv, patch, width_index):
        return pltpu.make_async_remote_copy(
            src_ref=src,
            dst_ref=dst,
            send_sem=send,
            recv_sem=recv,
            device_id={"patch": patch, "width": width_index},
            device_id_type=MESH,
        )

    at_sender, at_edge, at_receiver, at_wo, at_node, at_aggregate, at_vo = (
        slice(k * width, (k + 1) * width) for k in range(7)
    )

    def weight(source, layer, first_column, target, count=1):
        from_ = source.at[layer, :, pl.ds(first_column, count * width)]
        to = weights.at[layer, here, pl.ds(target.start, count * width)]
        return from_, to

    def layer_rest(layer):
        return [
            weight(wo_in, layer, 0, at_wo),
            weight(vi_in, layer, 0, at_node, 2),
            weight(vo_in, layer, 0, at_vo),
        ]

    def layer_ends(layer):
        return [
            weight(wi_in, layer, 0, at_edge),
            weight(wi_in, layer, 2 * width, at_receiver),
        ]

    groups = [
        ("nodes", [(nodes_in, nodes.at[here])], nodes.at[there]),
        ("sender", [weight(wi_in, 0, width, at_sender)], weights.at[0, there, at_sender]),
        ("ends", layer_ends(0), weights.at[0, there, pl.ds(width, 2 * width)]),
        ("edges", None, edges.at[there]),
        (
            "vectors",
            [(source, vectors.at[index, :, here]) for index, source in enumerate(vector_in)],
            vectors.at[:, :, there],
        ),
        ("rest", layer_rest(0), weights.at[0, there, pl.ds(3 * width, 4 * width)]),
    ]
    for layer in range(1, layers):
        groups.append(
            (
                layer,
                [weight(wi_in, layer, width, at_sender)] + layer_ends(layer) + layer_rest(layer),
                weights.at[layer, there],
            )
        )
    place = {group[0]: index for index, group in enumerate(groups)}
    send_of = {"nodes": 0, "edges": 1, "vectors": 2}
    mine_of = {
        "nodes": nodes.at[here],
        "sender": weights.at[0, here, at_sender],
        "ends": weights.at[0, here, pl.ds(width, 2 * width)],
        "edges": edges.at[here],
        "vectors": vectors.at[:, :, here],
        "rest": weights.at[0, here, pl.ds(3 * width, 4 * width)],
    } | {layer: weights.at[layer, here] for layer in range(1, layers)}

    barrier = pltpu.get_barrier_semaphore()

    @pl.when(core == lead)
    def _():
        pl.semaphore_signal(barrier, inc=1, device_id={"patch": me, "width": other}, device_id_type=MESH)

    def greet(step, carry):
        target = lax.rem(me + step, patches)

        @pl.when((target != 0) | (me == 1))
        def _():
            pl.semaphore_signal(
                pltpu.get_barrier_semaphore(),
                inc=1,
                device_id={"patch": target, "width": lead},
                device_id_type=MESH,
            )

        return carry

    lax.fori_loop(1, patches, greet, 0)

    count_copy = pltpu.make_async_copy(count_in, count_ref, graph_sem.at[1])
    graph_copies = [
        pltpu.make_async_copy(source, graph_ref.at[pl.ds(k, 1)], graph_sem.at[0])
        for k, source in enumerate((senders_in, receivers_in))
    ]

    def locals_of(index):
        name, copies, _ = groups[index]
        if name == "edges":
            copies = [(edges_in.at[:, my_slots], edges.at[here])]
        return [pltpu.make_async_copy(source, target, local_sem.at[index]) for source, target in copies]

    for index in range(2):
        for copy in locals_of(index):
            copy.start()
    for copy in [count_copy] + graph_copies:
        copy.start()
    for index in range(2, len(groups)):
        for copy in locals_of(index):
            copy.start()

    @pl.when(core != lead)
    def _():
        pl.semaphore_wait(barrier, 1)
        pl.semaphore_signal(mate, inc=1, device_id={"patch": me, "width": lead}, device_id_type=MESH)

    @pl.when(core == lead)
    def _():
        pl.semaphore_wait(mate, 1)

    for index, (name, copies, _) in enumerate(groups):
        if name == "edges":
            copies = [(edges_in.at[:, other_slots], edges.at[here])]
        for source, target in copies:
            remote(source, target, w_send.at[send_of.get(name, 3)], w_recv.at[index], me, other).start()

    def local_arrive(name):
        ref = mine_of[name]
        pltpu.make_async_copy(ref, ref, local_sem.at[place[name]]).wait()

    def arrive(name):
        if name not in ("nodes", "sender"):
            local_arrive(name)
        ref = groups[place[name]][2]
        remote(ref, ref, w_send.at[send_of.get(name, 3)], w_recv.at[place[name]], me, other).wait_recv()

    def hot(index, iota):
        return jnp.where(iota == index, 1.0, 0.0).astype(bf16)

    def masks():
        count_copy.wait()
        pltpu.make_async_copy(graph_ref, graph_ref, graph_sem.at[0]).wait()
        sender = graph_ref[0:1, my_slots]
        receiver = graph_ref[1:2, my_slots] - me * rows
        slot = lax.broadcasted_iota(jnp.int32, (1, mine), 1) + core * mine
        live = slot < count_ref[0]
        owner = sender // rows
        within = sender - owner * rows
        distance = lax.rem(me - owner + patches, patches)
        node_iota = lax.broadcasted_iota(jnp.int32, (rows, mine), 0)
        hot_own[:rows] = hot(jnp.where(distance == 0, within, -1), node_iota)
        hot_own[rows:] = hot(receiver, node_iota)
        hot_far[:rows] = hot(jnp.where(distance == 1, within, -1), node_iota)
        hot_far[rows : 2 * rows] = hot(jnp.where(distance == patches - 1, within, -1), node_iota)
        far_index = jnp.where((distance >= 2) & (distance <= patches - 2), (distance - 2) * top + within, -1)
        hot_far[2 * rows :] = hot(far_index, lax.broadcasted_iota(jnp.int32, (coarse.shape[1], mine), 0))
        incidence[...] = hot(jnp.where(live, receiver, -1), node_iota)
        return live

    pad = coarse.shape[1] - far * top
    if pad:
        for layer in range(layers):
            coarse[layer, far * top :, :] = jnp.zeros((pad, width), bf16)

    def halo_part(layer, side):
        return halo.at[layer, :, pl.ds(pl.multiple_of(side * rows, rows), rows)]

    def halo_copy(layer, side):
        return remote(
            part_send.at[layer],
            halo_part(layer, side),
            halo_send.at[layer],
            halo_recv.at[layer, side],
            lax.rem(me + 1 + side * (patches - 2), patches),
            lead,
        )

    def halo_arrival(layer, side):
        ref = halo_part(layer, side)
        return remote(ref, ref, halo_send.at[layer], halo_recv.at[layer, side], me, other)

    def coarse_part(layer):
        return coarse.at[layer, pl.ds(0, far * top)]

    def spread_coarse(layer):
        def send(target, step):
            remote(
                coarse_send.at[layer],
                coarse.at[layer, pl.ds(pl.multiple_of((step - 2) * top, top), top)],
                coarse_send_sem.at[layer],
                coarse_recv_sem.at[layer],
                target,
                1 - lead,
            ).start()

        def spread(turn, carry):
            step = patches - 2 - turn
            pl.when(me + step < patches)(lambda: send(me + step, step))
            pl.when(me - step >= 0)(lambda: send(me - step, patches - step))
            return carry

        lax.fori_loop(0, far, spread, 0)

    def send_halo(layer):
        if layer == 0:
            pl.semaphore_wait(barrier, jnp.where(me == 0, 2, 2 * (patches - 1)))

            @pl.when(me != 0)
            def _():
                pl.semaphore_signal(
                    all_in, inc=1, device_id={"patch": me, "width": other}, device_id_type=MESH
                )

            @pl.when(me == 1)
            def _():
                pl.semaphore_signal(all_in, inc=1, device_id={"patch": 0, "width": other}, device_id_type=MESH)
                halo_arrival(0, 0).wait_recv()
                remote(
                    halo_part(0, 0), halo_part(0, 1), halo_send.at[0], halo_recv.at[0, 1], patches - 1, lead
                ).start()

            pl.when(me != 0)(halo_copy(0, 1 - odd).start)
        else:
            halo_copy(layer, 1 - odd).start()
        halo_copy(layer, odd).start()

    def send_coarse(layer):
        if layer == 0:
            pl.semaphore_wait(all_in, 1)
        spread_coarse(layer)

    def column(index, layer):
        position = index * layers + layer
        return columns[:, position : position + 1]

    wide = [(k * mine // 2, (k + 1) * mine // 2) for k in range(2)]
    for layer in range(layers):
        if layer == 0:
            local_arrive("nodes")
            local_arrive("sender")
            arrive("nodes")
            arrive("sender")
        else:
            arrive(layer)
        part = dot(weights[layer, :, at_sender], nodes[...])
        part_send[layer] = part.astype(bf16)
        coarse_send[layer] = part.T[:top].astype(bf16)
        pl.when(core == lead)(functools.partial(send_halo, layer))
        pl.when(core != lead)(functools.partial(send_coarse, layer))
        if layer == 0:
            live = masks()
            arrive("ends")
        own[:, :rows] = part.astype(bf16)
        own[:, rows:] = dot(weights[layer, :, at_receiver], nodes[...]).astype(bf16)
        if layer == 0:
            arrive("edges")
            arrive("vectors")
            flat = vectors[...].reshape(8 * layers, width)
            columns[...] = flat.T
        before[...] = (
            dot(weights[layer, :, at_edge], edges[...]) + dot(own[...], hot_own[...]) + column(0, layer)
        )
        if layer == 0:
            arrive("rest")
        node_first = dot(weights[layer, :, at_node], nodes[...]) + column(4, layer)
        wo_turned[...] = weights[layer, :, at_wo].T
        vo_turned[...] = weights[layer, :, at_vo].T

        every = coarse_part(layer)
        all_coarse = remote(
            every, every, coarse_send_sem.at[layer], coarse_recv_sem.at[layer], me, other
        )

        def relay(ref):
            return remote(ref, ref, relay_send.at[layer], relay_recv.at[layer], me, other)

        def near_term(low, high):
            return dot(halo[layer], hot_far[: 2 * rows, low:high])

        def away_term(low, high):
            return dot(coarse[layer], hot_far[2 * rows :, low:high], ((0,), (0,)))

        def edge_phase(last_term):
            total = None
            for low, high in wide:
                hidden = silu(before[:, low:high] + last_term(low, high)).astype(bf16)
                mlp = dot(wo_turned[...], hidden) + column(1, layer)
                updated = edges[:, low:high].astype(f32) + layer_norm(mlp, column(2, layer), column(3, layer))
                fresh = jnp.where(live[:, low:high], updated, 0.0).astype(bf16)
                edges[:, low:high] = fresh
                term = dot(fresh, incidence[:, low:high], ((1,), (1,)))
                total = term if total is None else total + term
            partial[...] = total
            agg_send[layer] = total.astype(bf16)

        @pl.when(core == lead)
        def _():
            for side in (1, 0) if layer else (0, 1):
                if layer == 0 and side == 0:
                    pl.when(me != 1)(halo_arrival(0, 0).wait_recv)
                else:
                    halo_arrival(layer, side).wait_recv()
                relay(halo_part(layer, side)).start()
            before[...] = before[...] + near_term(0, mine)
            relay(every).wait_recv()
            edge_phase(away_term)

        @pl.when(core != lead)
        def _():
            all_coarse.wait_recv()
            relay(every).start()
            before[...] = before[...] + away_term(0, mine)
            relay(halo.at[layer]).wait_recv()
            edge_phase(near_term)

        swap = remote(
            agg_send.at[layer], agg_recv.at[layer], agg_sems.at[layer, 0], agg_sems.at[layer, 1], me, other
        )
        swap.start()
        if layer == layers - 1:
            keep = pltpu.make_async_copy(edges.at[here], edges_out.at[:, my_slots], out_sems.at[0])
            keep.start()
            give = remote(
                edges.at[there], edges_out.at[:, my_slots], out_sems.at[1], out_sems.at[2], me, other
            )
            give.start()
        swap.wait_recv()
        aggregate = (partial[...] + agg_recv[layer].astype(f32)).astype(bf16)
        node_hidden = silu(node_first + dot(weights[layer, :, at_aggregate], aggregate)).astype(bf16)
        node_mlp = dot(vo_turned[...], node_hidden) + column(5, layer)
        nodes[...] = (
            nodes[...].astype(f32) + layer_norm(node_mlp, column(6, layer), column(7, layer))
        ).astype(bf16)
        swap.wait_send()

    nodes_out[...] = nodes[here, :]
    for ref, index in ((nodes.at[here], 0), (edges.at[here], 1), (vectors.at[:, :, here], 2), (weights.at[:, here], 3)):
        remote(ref, ref, w_send.at[index], w_recv.at[index], me, other).wait_send()

    def sent(ref, sem):
        remote(ref, ref, sem, w_recv.at[0], me, other).wait_send()

    @pl.when(core == lead)
    def _():
        for layer in range(layers):
            sent(halo.at[layer], relay_send.at[layer])
        for layer in range(1, layers):
            sent(halo.at[layer], halo_send.at[layer])
        one = part_send.at[0]
        pl.when(me == 0)(lambda: sent(one, halo_send.at[0]))
        pl.when(me == 1)(lambda: sent(weights.at[0, :, pl.ds(0, 3 * rows)], halo_send.at[0]))
        pl.when(me > 1)(lambda: sent(halo.at[0], halo_send.at[0]))

    @pl.when(core != lead)
    def _():
        for layer in range(layers):
            sent(coarse_part(layer), relay_send.at[layer])
            sent(coarse_part(layer), coarse_send_sem.at[layer])

    keep.wait()
    give.wait_send()
    got = edges_out.at[:, other_slots]
    remote(got, got, out_sems.at[1], out_sems.at[2], me, other).wait_recv()


def put(nodes, edges, nodes_out, edges_out, sems):
    copies = [
        pltpu.make_async_copy(edges, edges_out, sems.at[0]),
        pltpu.make_async_copy(nodes, nodes_out, sems.at[1]),
    ]
    for copy in copies:
        copy.start()
    for copy in copies:
        copy.wait()


def on_device(
    patches,
    node_latents,
    edge_latents,
    senders,
    receivers,
    edge_count,
    edge_in_weight,
    edge_in_bias,
    edge_out_weight,
    edge_out_bias,
    edge_gain,
    edge_shift,
    node_in_weight,
    node_in_bias,
    node_out_weight,
    node_out_bias,
    node_gain,
    node_shift,
):
    half, rows = node_latents.shape
    slots = edge_latents.shape[1]
    layers = edge_in_weight.shape[0]
    width = 2 * half
    mine = slots // 2
    top = rows // 8
    far_rows = -(-(patches - 3) * top // 128) * 128
    vmem = pltpu.VMEM
    dma = pltpu.SemaphoreType.DMA
    groups = 5 + layers
    anywhere = pl.BlockSpec(memory_space=pl.ANY)
    results = pl.pallas_call(
        functools.partial(kernel, patches),
        out_shape=(
            vmem((half, rows), bf16),
            vmem((half, slots), bf16),
        ),
        in_specs=[anywhere] * 17,
        out_specs=(pl.BlockSpec(memory_space=vmem),) * 2,
        scratch_shapes=[
            vmem((width, rows), bf16),
            vmem((width, mine), bf16),
            vmem((layers, width, 7 * width), bf16),
            vmem((8, layers, width), f32),
            vmem((width, 8 * layers), f32),
            vmem((layers, width, 2 * rows), bf16),
            vmem((layers, far_rows, width), bf16),
            vmem((layers, width, rows), bf16),
            vmem((layers, top, width), bf16),
            vmem((layers, width, rows), bf16),
            vmem((layers, width, rows), bf16),
            vmem((width, rows), f32),
            vmem((width, 2 * rows), bf16),
            vmem((2 * rows, mine), bf16),
            vmem((2 * rows + far_rows, mine), bf16),
            vmem((rows, mine), bf16),
            vmem((width, mine), f32),
            vmem((2, slots), jnp.int32),
            pltpu.SMEM((1,), jnp.int32),
            vmem((width, width), bf16),
            vmem((width, width), bf16),
            dma((2,)),
            dma((groups,)),
            dma((4,)),
            dma((groups,)),
            dma((layers,)),
            dma((layers, 2)),
            dma((layers,)),
            dma((layers,)),
            dma((layers,)),
            dma((layers,)),
            dma((layers, 2)),
            dma((3,)),
            pltpu.SemaphoreType.REGULAR,
            pltpu.SemaphoreType.REGULAR,
        ],
        compiler_params=pltpu.CompilerParams(collective_id=0, has_side_effects=True, vmem_limit_bytes=56 * 2**20),
    )(
        node_latents,
        edge_latents,
        senders.reshape(1, slots),
        receivers.reshape(1, slots),
        edge_count,
        edge_in_weight,
        edge_out_weight,
        node_in_weight,
        node_out_weight,
        edge_in_bias,
        edge_out_bias,
        edge_gain,
        edge_shift,
        node_in_bias,
        node_out_bias,
        node_gain,
        node_shift,
    )
    return pl.pallas_call(
        put,
        out_shape=(
            jax.ShapeDtypeStruct((half, rows), bf16),
            jax.ShapeDtypeStruct((half, slots), bf16),
        ),
        in_specs=[pl.BlockSpec(memory_space=vmem)] * 2,
        out_specs=(anywhere, anywhere),
        scratch_shapes=[dma((2,))],
        compiler_params=pltpu.CompilerParams(vmem_limit_bytes=4 * 2**20),
    )(*results)


def solution(mesh):
    by_width = P(None, "width")
    return jax.shard_map(
        functools.partial(on_device, mesh.shape["patch"]),
        mesh=mesh,
        in_specs=(
            P("width", "patch"),
            P("width", "patch"),
            P("patch"),
            P("patch"),
            P("patch"),
            P(None, "width", None),
            by_width,
            P(None, "width", None),
            by_width,
            by_width,
            by_width,
            P(None, "width", None),
            by_width,
            P(None, "width", None),
            by_width,
            by_width,
            by_width,
        ),
        out_specs=(P("width", "patch"), P("width", "patch")),
        check_vma=False,
    )
```

time: 31.6 us -> 30.5 us (0.965)
  Pallas kernels: 30.2 us -> 29.1 us
    pallas_call x1, Pallas kernels: 29.3 us -> 28.3 us  [on_device(): pl.pallas_call(functools.partial(kernel, patches), out_shape=(vmem((half,...]
where the time goes in v1:
time: 30.5 us; the launch traced here: 30.4 us
  Pallas kernels  29.1 us (95%)
  between operations  1.29 us (4%)
    pallas_call x1, Pallas kernels, on_device(): pl.pallas_call(functools.partial(kernel, patches), out_shape=(vmem((half,...  28.3 us
    pallas_call x1, Pallas kernels, on_device(): pl.pallas_call(put, out_shape=(jax.ShapeDtypeStruct((half, rows), bf16),...  0.82 us

profile of v1, /device:TPU:0, one launch (start us, length us, event | category | flops | bytes accessed | tf_op | source)
XLA Modules:
  0.0 30.4 jit_solution(11177102640614412866)
XLA Ops:
  1.3 28.3 %shard_map.176 = (bf16[256,128]{1,0:T(8,128)(2,1)S(1)}, bf16[256,1024]{1,0:T(8,128)(2,1)S(1)}) custom-call(bf16[256,128]{1,0:T(8,128)(2,1)} %nodes_in.1, bf16[256,1024]{1,0:T(8,128)(2,1)} %edges_in.1, s32[1,1024]{1,0:T(1,128)} %bitcast.2, s32[1,1024]{1,0:T(1,128)} %bitcast.3, s32[1]{0:T(128)S(6)} %copy.19.count_in, bf16[2,256,1536]{2,1,0:T(8,128)(2,1)} %wi_in.1, ...), custom_call_target="tpu_custom_call" | custom-call | tf_op jit(solution)/shard_map/pallas_call | solution.py:505
  29.6 0.8 %shard_map.177 = (bf16[256,128]{1,0:T(8,128)(2,1)}, bf16[256,1024]{1,0:T(8,128)(2,1)}) custom-call(bf16[256,128]{1,0:T(8,128)(2,1)S(1)} %get-tuple-element.4.nodes, bf16[256,1024]{1,0:T(8,128)(2,1)S(1)} %get-tuple-element.5.edges), custom_call_target="tpu_custom_call" | custom-call | tf_op jit(solution)/shard_map/pallas_call | solution.py:570
